TPU v7x, 32 devices: a whole 2x2x4 slice. The times are simulated.
32 devices in a mesh: dp: 8 (over y, x, core), own: 4 (over z).
Axes of the slice: x: 2, y: 2, z: 4, core: 2. Of those that a mesh axis runs over, the one named last changes fastest.
Arguments:
- grad: bfloat16 [8192, 1024], P(('dp', 'own')), may hold values from -88 to 88
- left_stats: float32 [8, 1024, 1024], P('dp', 'own'), may hold values from -0.4 to 2.6
- right_stats: float32 [8, 1024, 1024], P('dp', 'own'), may hold values from -0.4 to 2.6
- left_roots: float32 [8, 1024, 1024], P('dp', 'own'), may hold values from -0.4 to 2.6, as said below
- right_roots: float32 [8, 1024, 1024], P('dp', 'own'), may hold values from -0.4 to 2.6, as said below
Outputs:
- direction: bfloat16 [8192, 1024], P(('dp', 'own'))
- left_new: float32 [8, 1024, 1024], P('dp', 'own')
- right_new: float32 [8, 1024, 1024], P('dp', 'own')
Inputs may be any that keep to these rules, and one draw needn't show every extreme that they name: `right_roots`: each block's feature-side root is symmetric. `left_roots`: each block's vocabulary-side root is symmetric.
All inputs are finite; a program needn't handle non-finite values.
Results may differ from a plain program's by a relative error of at most 0.0049.
Values may be sent and summed in bfloat16 or wider, within the bound.
No kernel may reach another device: no remote copies, remote signals or barrier semaphores. Data moves between devices by JAX's collectives and lax.ppermute only.
A program may use at most 64 MiB of HBM per device.

v0:
```python
import jax
import jax.numpy as jnp
from jax import lax
from jax.sharding import PartitionSpec as P

highest = lax.Precision.HIGHEST
epsilon = 1e-06


def transpose_product(left_side, right_side):
    return lax.dot_general(
        left_side, right_side, (((0,), (0,)), ((), ())), preferred_element_type=jnp.float32
    )


def local(grad, left_stats, right_stats, left_roots, right_roots):
    feature_width = grad.shape[1]
    owner_count = lax.axis_size("own")
    slice_width = feature_width // owner_count
    own_rows = grad.astype(jnp.float32)
    grad_square = jnp.sum(own_rows * own_rows)
    whole_grad = lax.all_gather(grad, "own", axis=0, tiled=True)
    feature_cols = lax.dynamic_slice_in_dim(
        whole_grad, lax.axis_index("own") * slice_width, slice_width, 1
    )
    left_gram = lax.dot_general(
        grad, whole_grad, (((1,), (1,)), ((), ())), preferred_element_type=jnp.float32
    )
    right_gram = transpose_product(feature_cols, whole_grad)
    left_update = 0.9 * left_stats[0] + 0.1 / feature_width * left_gram
    right_update = 0.9 * right_stats[0] + 0.1 / feature_width * right_gram
    mixed_cols = lax.dot_general(
        whole_grad.astype(jnp.float32), right_roots[0], (((1,), (1,)), ((), ())), precision=highest
    )
    mixed_cols = mixed_cols.astype(jnp.bfloat16)
    precond = jnp.dot(
        left_roots[0],
        lax.all_gather(mixed_cols, "own", axis=1, tiled=True).astype(jnp.float32),
        precision=highest,
    )
    precond_square = jnp.sum(precond * precond)
    norm_totals = lax.psum((grad_square, precond_square), "own")
    graft_scale = jnp.sqrt(norm_totals[0] / (norm_totals[1] + epsilon))
    direction = (precond * graft_scale).astype(jnp.bfloat16)
    return (direction, left_update[None], right_update[None])


def solution(mesh):
    in_specs = (
        P(("dp", "own"), None),
        P("dp", "own", None),
        P("dp", "own", None),
        P("dp", "own", None),
        P("dp", "own", None),
    )
    out_specs = (P(("dp", "own"), None), P("dp", "own", None), P("dp", "own", None))
    return jax.shard_map(local, mesh=mesh, in_specs=in_specs, out_specs=out_specs, check_vma=False)
```

profile of v0, /device:TPU:0, one launch (start us, length us, event | category | flops | bytes accessed | tf_op | source)
XLA Modules:
  0.0 131.7 jit_solution(18139367668326251888)
XLA Ops:
  7.2 0.0 copy-start
  7.2 0.0 all-gather.3.cloned.1.call-start
  7.2 0.7 all-gather.3.cloned.1.call-update
  7.9 0.0 all-gather.5.cloned.1.call-start
  8.0 50.0 %all-gather.3.cloned.1.call-done = bf16[1024,1024]{1,0:T(8,128)(2,1)} async-done(((bf16[256,1024]{1,0:T(8,128)(2,1)}), bf16[1024,1024]{1,0:T(8,128)(2,1)}) %all-gather.3.cloned.1.call-update) | async-done | bytes 2097168 | tf_op jit(solution)/shard_map/all_gather | solution.py:22
  58.0 0.0 copy-start.1
  58.0 4.7 %convolution_convert_fusion = bf16[1024,256]{1,0:T(8,128)(2,1)} fusion(bf16[1024,1024]{1,0:T(8,128)(2,1)} %all-gather.3.cloned.1.call-done, f32[1,256,1024]{2,1,0:T(8,128)} %param.9), kind=kOutput, calls=%fused_computation.6 | convolution fusion | flops 3221487616 | bytes 3670016 | tf_op jit(solution)/shard_map/dot_general | solution.py:32
  62.6 0.0 all-gather.5.cloned.1.call-update
  62.7 1.9 %multiply_reduce_fusion.1 = f32[]{:T(128)} fusion(bf16[256,1024]{1,0:T(8,128)(2,1)} %param.5), kind=kLoop, calls=%fused_computation.12 | loop fusion | flops 786431 | bytes 524292 | tf_op jit(solution)/shard_map/reduce_sum | solution.py:21
  64.6 0.0 copy-done.1
  64.6 0.0 copy-start.2
  64.6 0.0 copy-start.3
  64.6 3.1 %fusion.1 = f32[1,256,1024]{2,1,0:T(8,128)} fusion(bf16[1024,1024]{1,0:T(8,128)(2,1)S(1)} %copy-done.1, f32[1,256,1024]{2,1,0:T(8,128)} %param.7, s32[]{:T(128)S(6)} %select_n.3), kind=kOutput, calls=%fused_computation.2 | convolution fusion | flops 537657344 | bytes 4718596 | tf_op jit(solution)/shard_map/dot_general | solution.py:11
  67.7 0.0 copy-done.2
  67.7 0.0 copy-done.3
  67.7 1.8 %fusion.3 = f32[1,256,1024]{2,1,0:T(8,128)} fusion(bf16[256,1024]{1,0:T(8,128)(2,1)S(1)} %copy-done.2, bf16[1024,1024]{1,0:T(8,128)(2,1)S(1)} %copy-done.1, f32[1,256,1024]{2,1,0:T(8,128)S(1)} %copy-done.3), kind=kOutput, calls=%fused_computation.5 | convolution fusion | flops 537657344 | bytes 4718592 | tf_op jit(solution)/shard_map/dot_general | solution.py:26
  69.4 38.4 %all-gather.5.cloned.1.call-done = bf16[1024,1024]{1,0:T(8,128)(2,1)} async-done(((bf16[1024,256]{1,0:T(8,128)(2,1)}), bf16[1024,1024]{1,0:T(8,128)(2,1)}) %all-gather.5.cloned.1.call-update) | async-done | bytes 2097168 | tf_op jit(solution)/shard_map/all_gather | solution.py:38
  107.9 0.0 copy-done
  107.9 4.6 %multiply_reduce_fusion = (f32[]{:T(128)}, f32[1024,256]{1,0:T(8,128)S(1)}) fusion(bf16[1024,1024]{1,0:T(8,128)(2,1)} %all-gather.5.cloned.1.call-done, f32[1,256,1024]{2,1,0:T(8,128)S(1)} %copy-done), kind=kOutput, calls=%fused_computation.11 | convolution fusion | flops 3221749760 | bytes 4194308 | tf_op jit(solution)/shard_map/dot_general | solution.py:36
  112.4 10.0 %all-reduce = (f32[]{:T(128)}, f32[]{:T(128)}) all-reduce(f32[]{:T(128)} %multiply_reduce_fusion.1, f32[]{:T(128)} %get-tuple-element.8), channel_id=1, replica_groups=mesh['dp'=8,'own'=4] {'own'}, use_global_device_ids=true, to_apply=%region_1.0 | all-reduce | flops 2 | bytes 16 | tf_op jit(solution)/shard_map/psum | solution.py:42
  123.7 0.1 fusion.7
  123.9 1.0 copy.8
Async XLA Ops:
  7.2 100.7 %copy-start = (f32[1,256,1024]{2,1,0:T(8,128)S(1)}, f32[1,256,1024]{2,1,0:T(8,128)}, u32[]{:S(2)}) copy-start(f32[1,256,1024]{2,1,0:T(8,128)} %param.8) | copy-start | bytes 3145732
  7.2 50.8 %all-gather.3.cloned.1.call-start = ((), (), s32[]{:S(2)}) async-start(), calls=%async_computation | async-start | bytes 2621440 | tf_op jit(solution)/shard_map/all_gather | solution.py:22
  7.9 100.0 %all-gather.5.cloned.1.call-start = ((), (), s32[]{:S(2)}) async-start(), calls=%async_computation.1 | async-start | bytes 2621440 | tf_op jit(solution)/shard_map/all_gather | solution.py:38
  58.0 6.6 %copy-start.1 = (bf16[1024,1024]{1,0:T(8,128)(2,1)S(1)}, bf16[1024,1024]{1,0:T(8,128)(2,1)}, u32[]{:S(2)}) copy-start(bf16[1024,1024]{1,0:T(8,128)(2,1)} %all-gather.3.cloned.1.call-done) | copy-start | bytes 6291460
  64.6 3.1 %copy-start.2 = (bf16[256,1024]{1,0:T(8,128)(2,1)S(1)}, bf16[256,1024]{1,0:T(8,128)(2,1)}, u32[]{:S(2)}) copy-start(bf16[256,1024]{1,0:T(8,128)(2,1)} %param.5) | copy-start | bytes 1572868
  64.6 3.1 %copy-start.3 = (f32[1,256,1024]{2,1,0:T(8,128)S(1)}, f32[1,256,1024]{2,1,0:T(8,128)}, u32[]{:S(2)}) copy-start(f32[1,256,1024]{2,1,0:T(8,128)} %param.6) | copy-start | bytes 3145732
Sparse Core Ops, SparseCore 0:
  9.6 48.3 all-gather.2
  62.8 45.0 all-gather.4
where the time goes:
time: 132 us
  waiting for transfers between devices  89.2 us (68%)
  between operations  15.3 us (12%)
  matrix products  14.1 us (11%)
  blocking collectives  10 us (8%)
  other arithmetic  2.01 us (2%)
    all_gather x1, waiting for transfers between devices, local(): whole_grad = lax.all_gather(grad, 'own', axis=0, tiled=True)  50 us
    all_gather x1, waiting for transfers between devices, local(): lax.all_gather(mixed_cols, 'own', axis=1, tiled=True).astype(jnp.float32)  38.4 us
    psum x1, blocking collectives, local(): norm_totals = lax.psum((grad_square, precond_square), 'own')  10 us
    dot_general x1, matrix products, local(): lax.dot_general(whole_grad.astype(jnp.float32), right_roots[0], (((1,), (...  4.66 us
    dot_general x1, matrix products, local(): jnp.dot(left_roots[0], lax.all_gather(mixed_cols, 'own', axis=1, tiled=Tr...  4.57 us
    dot_general x1, matrix products, transpose_product(): lax.dot_general(left_side, right_side, (((0,), (0,)), ((), ())), preferre...  3.07 us
  transfers between devices with their start and end apart: 2, of which 2 were waited for; matrix products, arithmetic and copies ran while one was open for 5% of the time, Pallas kernels for 0%

commit v1 on v0

--- a/solution.py
+++ b/solution.py
@@ -5,6 +5,16 @@
 
 highest = lax.Precision.HIGHEST
 epsilon = 1e-06
+
+
+def gather_by_hops(x, axis, along):
+    size = lax.axis_size(axis)
+    block, blocks = (x, [x])
+    for _ in range(size - 1):
+        block = lax.ppermute(block, axis, [(i, (i + 1) % size) for i in range(size)])
+        blocks.insert(0, block)
+    merged = jnp.concatenate(blocks, axis=along)
+    return jnp.roll(merged, (lax.axis_index(axis) + 1) * x.shape[along], axis=along)
 
 
 def transpose_product(left_side, right_side):
@@ -19,7 +29,7 @@
     slice_width = feature_width // owner_count
     own_rows = grad.astype(jnp.float32)
     grad_square = jnp.sum(own_rows * own_rows)
-    whole_grad = lax.all_gather(grad, "own", axis=0, tiled=True)
+    whole_grad = gather_by_hops(grad, "own", 0)
     feature_cols = lax.dynamic_slice_in_dim(
         whole_grad, lax.axis_index("own") * slice_width, slice_width, 1
     )

time: 132 us -> 128 us (0.970)
  waiting for transfers between devices: 89.2 us -> 71.7 us
  local copies, waits for them, and re-layouts: 1.02 us -> 12.2 us
  starting transfers between devices: 0.08 us -> 3.15 us
    all_gather x1 -> x0, waiting for transfers between devices: 50 us -> none  [local(): whole_grad = lax.all_gather(grad, 'own', axis=0, tiled=True)]
    ppermute x0 -> x3, waiting for transfers between devices: none -> 43.1 us  [gather_by_hops(): lax.ppermute(block, axis, [(i, (i + 1) % size) for i in range(size)])]
    unnamed x9 -> x20, local copies, waits for them, and re-layouts: 1.02 us -> 12.2 us
    all_gather x1, waiting for transfers between devices: 38.4 us -> 28.7 us  [local(): lax.all_gather(mixed_cols, 'own', axis=1, tiled=True).astype(jnp.float32)]
    ppermute x0 -> x3, starting transfers between devices: none -> 3.11 us  [gather_by_hops(): lax.ppermute(block, axis, [(i, (i + 1) % size) for i in range(size)])]
    dot_general x1, matrix products: 4.66 us -> 2.66 us  [local(): lax.dot_general(whole_grad.astype(jnp.float32), right_roots[0], (((1,), (...]
    dot_general x1, matrix products: 1.77 us -> 3.37 us  [local(): lax.dot_general(grad, whole_grad, (((1,), (1,)), ((), ())), preferred_ele...]
  transfers between devices with their start and end apart: 2 -> 4, of which waited for: 2 -> 4; matrix products, arithmetic and copies ran while one was open for 5% -> 12% of each run, Pallas kernels for 0% -> 0%
where the time goes in v1:
time: 128 us
  waiting for transfers between devices  71.7 us (56%)
  between operations  15.5 us (12%)
  matrix products  13.8 us (11%)
  local copies, waits for them, and re-layouts  12.2 us (10%)
  blocking collectives  10.1 us (8%)
  starting transfers between devices  3.15 us (2%)
    ppermute x3, waiting for transfers between devices, gather_by_hops(): lax.ppermute(block, axis, [(i, (i + 1) % size) for i in range(size)])  43.1 us
    all_gather x1, waiting for transfers between devices, local(): lax.all_gather(mixed_cols, 'own', axis=1, tiled=True).astype(jnp.float32)  28.7 us
    unnamed x20, local copies, waits for them, and re-layouts  12.2 us
    psum x1, blocking collectives, local(): norm_totals = lax.psum((grad_square, precond_square), 'own')  10.1 us
    dot_general x1, matrix products, local(): jnp.dot(left_roots[0], lax.all_gather(mixed_cols, 'own', axis=1, tiled=Tr...  4.56 us
    dot_general x1, matrix products, local(): lax.dot_general(grad, whole_grad, (((1,), (1,)), ((), ())), preferred_ele...  3.37 us
    dot_general x1, matrix products, transpose_product(): lax.dot_general(left_side, right_side, (((0,), (0,)), ((), ())), preferre...  3.24 us
    ppermute x3, starting transfers between devices, gather_by_hops(): lax.ppermute(block, axis, [(i, (i + 1) % size) for i in range(size)])  3.11 us
  transfers between devices with their start and end apart: 4, of which 4 were waited for; matrix products, arithmetic and copies ran while one was open for 12% of the time, Pallas kernels for 0%

profile of v1, /device:TPU:0, one launch (start us, length us, event | category | flops | bytes accessed | tf_op | source)
XLA Modules:
  0.0 127.6 jit_solution(6366069081329751119)
XLA Ops:
  7.2 0.0 copy-start
  7.2 0.0 copy-start.2
  7.2 0.0 all-gather.2.cloned.1.call-start
  7.2 3.1 %collective-permute-start = (bf16[256,1024]{1,0:T(8,128)(2,1)}, bf16[256,1024]{1,0:T(8,128)(2,1)S(1)}, u32[]{:S(2)}, u32[]{:S(2)}) collective-permute-start(bf16[256,1024]{1,0:T(8,128)(2,1)} %param.5), channel_id=1, source_target_pairs={{0,1},{1,2},{2,3},{3,0},{4,5},{5,6},{6,7},{7,4},{8,9},{9,10},{10,1... | collective-permute-start | bytes 1572872 | tf_op jit(solution)/shard_map/ppermute | solution.py:14
  10.3 14.2 %collective-permute-done = bf16[256,1024]{1,0:T(8,128)(2,1)S(1)} collective-permute-done((bf16[256,1024]{1,0:T(8,128)(2,1)}, bf16[256,1024]{1,0:T(8,128)(2,1)S(1)}, u32[]{:S(2)}, u32[]{:S(2)}) %collective-permute-start) | collective-permute-done | bytes 524320 | tf_op jit(solution)/shard_map/ppermute | solution.py:14
  24.5 0.0 collective-permute-start.1
  24.5 14.9 %collective-permute-done.1 = bf16[256,1024]{1,0:T(8,128)(2,1)S(1)} collective-permute-done((bf16[256,1024]{1,0:T(8,128)(2,1)S(1)}, bf16[256,1024]{1,0:T(8,128)(2,1)S(1)}, u32[]{:S(2)}, u32[]{:S(2)}) %collective-permute-start.1) | collective-permute-done | bytes 524320 | tf_op jit(solution)/shard_map/ppermute | solution.py:14
  39.4 0.0 collective-permute-start.2
  39.4 0.0 copy-start.3
  39.4 14.0 %collective-permute-done.2 = bf16[256,1024]{1,0:T(8,128)(2,1)S(1)} collective-permute-done((bf16[256,1024]{1,0:T(8,128)(2,1)S(1)}, bf16[256,1024]{1,0:T(8,128)(2,1)S(1)}, u32[]{:S(2)}, u32[]{:S(2)}) %collective-permute-start.2) | collective-permute-done | bytes 524320 | tf_op jit(solution)/shard_map/ppermute | solution.py:14
  53.5 1.1 constant_dynamic-update-slice_fusion.4
  54.8 0.0 copy-done.2
  54.8 0.0 copy-start.1
  54.8 1.9 %copy-done.1 = bf16[2048,1024]{1,0:T(8,128)(2,1)} copy-done((bf16[2048,1024]{1,0:T(8,128)(2,1)}, bf16[2048,1024]{1,0:T(8,128)(2,1)S(1)}, u32[]{:S(2)}) %copy-start.1) | copy-done | bytes 4194328
  56.8 0.0 copy-done.3
  56.8 2.7 %fusion.27 = bf16[1024,256]{1,0:T(8,128)(2,1)} fusion(bf16[2048,1024]{1,0:T(8,128)(2,1)S(1)} %constant_dynamic-update-slice_fusion, s32[]{:T(128)S(6)} %select_n.21, f32[1,256,1024]{2,1,0:T(8,128)S(1)} %copy-done.3), kind=kOutput, calls=%fused_computation.13 | convolution fusion | flops 3221487616 | bytes 3670020 | tf_op jit(solution)/shard_map/dot_general | solution.py:42
  59.4 0.0 all-gather.2.cloned.1.call-update
  59.5 1.6 %copy.8 = f32[1,256,1024]{1,2,0:T(8,128)S(1)} copy(f32[1,256,1024]{2,1,0:T(8,128)} %param.6) | data formatting | bytes 2097152 | tf_op args[1]
  61.0 2.6 %copy.9 = f32[1,256,1024]{1,2,0:T(8,128)} copy(f32[1,256,1024]{2,1,0:T(8,128)} %param.7) | data formatting | bytes 2097152 | tf_op args[2]
  63.6 0.9 multiply_reduce_fusion.1
  64.5 3.4 %fusion.15 = f32[1,256,1024]{1,2,0:T(8,128)} fusion(bf16[256,1024]{1,0:T(8,128)(2,1)S(1)} %copy-done.2, bf16[2048,1024]{1,0:T(8,128)(2,1)} %copy-done.1, s32[]{:T(128)S(6)} %select_n.21, f32[1,256,1024]{1,2,0:T(8,128)S(1)} %copy.8), kind=kOutput, calls=%fused_computation.9 | convolution fusion | flops 537657344 | bytes 4718596 | tf_op jit(solution)/shard_map/dot_general | solution.py:36
  67.9 2.5 %copy.12 = f32[1,256,1024]{2,1,0:T(8,128)} copy(f32[1,256,1024]{1,2,0:T(8,128)} %fusion.15) | data formatting | bytes 2097152
  70.4 3.2 %fusion.24 = f32[1,256,1024]{1,2,0:T(8,128)S(1)} fusion(bf16[2048,1024]{1,0:T(8,128)(2,1)} %copy-done.1, s32[]{:T(128)S(6)} %select_n.21, f32[1,256,1024]{1,2,0:T(8,128)} %copy.9, s32[]{:T(128)S(6)} %select_n.22, s32[]{:T(128)S(6)} %select_n.24), kind=kOutput, calls=%fused_computation.12 | convolution fusion | flops 537657344 | bytes 4718604 | tf_op jit(solution)/shard_map/dot_general | solution.py:21
  73.7 1.3 %copy.13 = f32[1,256,1024]{2,1,0:T(8,128)} copy(f32[1,256,1024]{1,2,0:T(8,128)S(1)} %fusion.24) | data formatting | bytes 2097152
  75.0 28.7 %all-gather.2.cloned.1.call-done = bf16[1024,1024]{1,0:T(8,128)(2,1)} async-done(((bf16[1024,256]{1,0:T(8,128)(2,1)}), bf16[1024,1024]{1,0:T(8,128)(2,1)}) %all-gather.2.cloned.1.call-update) | async-done | bytes 2097168 | tf_op jit(solution)/shard_map/all_gather | solution.py:48
  103.6 0.0 copy-done
  103.6 4.6 %multiply_reduce_fusion = (f32[]{:T(128)}, f32[1024,256]{1,0:T(8,128)S(1)}) fusion(bf16[1024,1024]{1,0:T(8,128)(2,1)} %all-gather.2.cloned.1.call-done, f32[1,256,1024]{2,1,0:T(8,128)S(1)} %copy-done), kind=kOutput, calls=%fused_computation.18 | convolution fusion | flops 3221749760 | bytes 4194308 | tf_op jit(solution)/shard_map/dot_general | solution.py:46
  108.2 10.1 %all-reduce = (f32[]{:T(128)}, f32[]{:T(128)}) all-reduce(f32[]{:T(128)} %multiply_reduce_fusion.1, f32[]{:T(128)} %get-tuple-element.8), channel_id=1, replica_groups=mesh['dp'=8,'own'=4] {'own'}, use_global_device_ids=true, to_apply=%region_1.2 | all-reduce | flops 2 | bytes 16 | tf_op jit(solution)/shard_map/psum | solution.py:52
  119.7 0.1 fusion.33
  119.8 1.0 copy.11
  (7 shorter events, 0.3 us)
Async XLA Ops:
  7.2 96.5 %copy-start = (f32[1,256,1024]{2,1,0:T(8,128)S(1)}, f32[1,256,1024]{2,1,0:T(8,128)}, u32[]{:S(2)}) copy-start(f32[1,256,1024]{2,1,0:T(8,128)} %param.8) | copy-start | bytes 3145732
  7.2 47.6 %copy-start.2 = (bf16[256,1024]{1,0:T(8,128)(2,1)S(1)}, bf16[256,1024]{1,0:T(8,128)(2,1)}, u32[]{:S(2)}) copy-start(bf16[256,1024]{1,0:T(8,128)(2,1)} %param.5) | copy-start | bytes 1572868
  7.2 96.4 %all-gather.2.cloned.1.call-start = ((), (), s32[]{:S(2)}) async-start(), calls=%async_computation | async-start | bytes 2621440 | tf_op jit(solution)/shard_map/all_gather | solution.py:48
  7.2 17.3 %collective-permute-start = (bf16[256,1024]{1,0:T(8,128)(2,1)}, bf16[256,1024]{1,0:T(8,128)(2,1)S(1)}, u32[]{:S(2)}, u32[]{:S(2)}) collective-permute-start(bf16[256,1024]{1,0:T(8,128)(2,1)} %param.5), channel_id=1, source_target_pairs={{0,1},{1,2},{2,3},{3,0},{4,5},{5,6},{6,7},{7,4},{8,9},{9,10},{10,1... | collective-permute-start | bytes 1572872 | tf_op jit(solution)/shard_map/ppermute | solution.py:14
  24.5 14.9 %collective-permute-start.1 = (bf16[256,1024]{1,0:T(8,128)(2,1)S(1)}, bf16[256,1024]{1,0:T(8,128)(2,1)S(1)}, u32[]{:S(2)}, u32[]{:S(2)}) collective-permute-start(bf16[256,1024]{1,0:T(8,128)(2,1)S(1)} %collective-permute-done), channel_id=1, source_target_pairs={{0,1},{1,2},{2,3},{3,0},{4,5},{5,6},{6,7},{7,4},{8,9},{9,10},{10,1... | collective-permute-start | bytes 1572872 | tf_op jit(solution)/shard_map/ppermute | solution.py:14
  39.4 14.0 %collective-permute-start.2 = (bf16[256,1024]{1,0:T(8,128)(2,1)S(1)}, bf16[256,1024]{1,0:T(8,128)(2,1)S(1)}, u32[]{:S(2)}, u32[]{:S(2)}) collective-permute-start(bf16[256,1024]{1,0:T(8,128)(2,1)S(1)} %collective-permute-done.1), channel_id=1, source_target_pairs={{0,1},{1,2},{2,3},{3,0},{4,5},{5,6},{6,7},{7,4},{8,9},{9,10},{10,1... | collective-permute-start | bytes 1572872 | tf_op jit(solution)/shard_map/ppermute | solution.py:14
  39.4 17.4 %copy-start.3 = (f32[1,256,1024]{2,1,0:T(8,128)S(1)}, f32[1,256,1024]{2,1,0:T(8,128)}, u32[]{:S(2)}) copy-start(f32[1,256,1024]{2,1,0:T(8,128)} %param.9) | copy-start | bytes 3145732
  54.8 1.9 %copy-start.1 = (bf16[2048,1024]{1,0:T(8,128)(2,1)}, bf16[2048,1024]{1,0:T(8,128)(2,1)S(1)}, u32[]{:S(2)}) copy-start(bf16[2048,1024]{1,0:T(8,128)(2,1)S(1)} %constant_dynamic-update-slice_fusion) | copy-start | bytes 12582916
Sparse Core Ops, SparseCore 0:
  59.6 44.0 all-gather.1
